TPU v7x, 32 devices: a whole 2x2x4 slice. The times are simulated.
32 devices in a mesh: section: 4 (over x, core), dp: 8 (over z, y).
Axes of the slice: x: 2, y: 2, z: 4, core: 2. Of those that a mesh axis runs over, the one named last changes fastest.
Arguments:
- hidden_in: bfloat16 [8, 512, 2048], P(None, 'dp'), may hold values from -8 to 8
- norm_gain: bfloat16 [4, 2048], P('section'), may hold values from 0.099609375 to 1.8984375
- router_weight: bfloat16 [4, 2048, 60], P('section'), may hold values from -1 to 1
- expert_scale: bfloat16 [4, 60, 2048], P('section'), may hold values from 1 to 16
- mix_weight: bfloat16 [4, 2048, 2048], P('section'), may hold values from -0.125 to 0.125
- routes: int32 [4, 8, 512, 4], P('section', None, 'dp'), may hold values from 0 to 59, as said below
Outputs:
- hidden_out: bfloat16 [8, 512, 2048], P('section', 'dp')
- balance_loss: float32 [4], P('section')
Inputs may be any that keep to these rules, and one draw needn't show every extreme that they name: `routes`: the 4 ids of a token in a layer are distinct.
All inputs are finite; a program needn't handle non-finite values.
Results may differ from a plain program's by a relative error of at most 0.01.
The roundings to bfloat16 on the way count: a program that leaves them out, or rounds other values in their place, can miss the bound.
Values may be sent and summed in bfloat16 or wider, within the bound.
A program may use at most 64 MiB of HBM per device.

v0:
```python
import jax
import jax.numpy as jnp
from jax import lax
from jax.sharding import PartitionSpec as P


def from_behind(block, axis, distance):
    devices = range(lax.axis_size(axis))
    route = [(i - distance, i) for i in devices if i - distance in devices]
    return lax.ppermute(block, axis, route)


def router_layer(hidden_rows, gain_row, w_router, scale_table, w_mix, chosen_ids):
    state_wide = hidden_rows.astype(jnp.float32)
    mean_square = jnp.mean(state_wide * state_wide, axis=-1, keepdims=True)
    normed = state_wide * lax.rsqrt(mean_square + 1e-06) * gain_row.astype(jnp.float32)
    logits = jnp.dot(normed.astype(jnp.bfloat16), w_router, preferred_element_type=jnp.float32)
    exponent = jnp.exp(logits)
    probabilities = exponent / jnp.sum(exponent, axis=-1, keepdims=True)
    expert_ids = jnp.arange(w_router.shape[1], dtype=jnp.int32)
    onehot = jnp.sum(
        (chosen_ids[:, :, None] == expert_ids[None, None, :]).astype(jnp.float32), axis=1
    )
    gate_values = (probabilities * onehot).astype(jnp.bfloat16)
    channel_scale = jnp.dot(gate_values, scale_table, preferred_element_type=jnp.float32)
    mixed_rows = (normed * channel_scale).astype(jnp.bfloat16)
    update = jnp.dot(mixed_rows, w_mix, preferred_element_type=jnp.float32)
    updated = (state_wide + update).astype(jnp.bfloat16)
    return (updated, jnp.sum(onehot, axis=0), jnp.sum(probabilities, axis=0))


def per_device(hidden_in, norm_gain, router_weight, expert_scale, mix_weight, routes):
    section_index = lax.axis_index("section")
    section_count = lax.axis_size("section")
    dp_count = lax.axis_size("dp")
    batches, tok_rows, width = hidden_in.shape
    experts = router_weight.shape[2]
    picks = routes.shape[3]
    group_size = 1
    group_count = batches // group_size
    group_rows = group_size * tok_rows
    step_count = group_count + section_count - 1
    grouped_routes = routes[0]

    def advance(step_index, carry):
        incoming, stored, count_total, prob_total = carry
        group_index = step_index - section_index
        active = (group_index >= 0) & (group_index < group_count)
        clipped = jnp.clip(group_index, 0, group_count - 1)
        fresh = lax.dynamic_index_in_dim(hidden_in, clipped, 0, keepdims=False)
        hidden_rows = jnp.where(section_index == 0, fresh, incoming)
        chosen_ids = lax.dynamic_index_in_dim(grouped_routes, clipped, 0, keepdims=False)
        updated, counts, prob_sums = router_layer(
            hidden_rows, norm_gain[0], router_weight[0], expert_scale[0], mix_weight[0], chosen_ids
        )
        weight_on = active.astype(jnp.float32)
        counts = counts * weight_on
        prob_sums = prob_sums * weight_on
        keep = active & (section_index == section_count - 1)
        previous = lax.dynamic_index_in_dim(stored, clipped, 0, keepdims=False)
        stored = lax.dynamic_update_index_in_dim(
            stored, jnp.where(keep, updated, previous), clipped, 0
        )
        incoming = from_behind(updated, "section", 1)
        return (incoming, stored, count_total + counts, prob_total + prob_sums)

    store_start = jnp.zeros((group_count, group_rows, width), jnp.bfloat16)
    initial = (
        jnp.zeros((group_rows, width), jnp.bfloat16),
        store_start,
        jnp.zeros((experts,), jnp.float32),
        jnp.zeros((experts,), jnp.float32),
    )
    incoming, stored, count_total, prob_total = lax.fori_loop(0, step_count, advance, initial)
    count_total, prob_total = lax.psum((count_total, prob_total), "dp")
    token_total = jnp.float32(batches * tok_rows * dp_count)
    fractions = count_total / (token_total * jnp.float32(picks))
    mean_probs = prob_total / token_total
    balance = jnp.float32(experts) * jnp.sum(fractions * mean_probs)
    balance_out = jnp.reshape(balance, (1,))
    terms = stored.astype(jnp.float32)
    delivered = lax.psum_scatter(
        terms.astype(jnp.bfloat16), "section", scatter_dimension=0, tiled=True
    )
    return (delivered, balance_out)


def solution(mesh):
    placed = (
        P(None, "dp", None),
        P("section", None),
        P("section", None, None),
        P("section", None, None),
        P("section", None, None),
        P("section", None, "dp", None),
    )
    return jax.shard_map(
        per_device,
        mesh=mesh,
        in_specs=placed,
        out_specs=(P("section", "dp", None), P("section")),
        check_vma=False,
    )
```

profile of v0, /device:TPU:3, one launch (start us, length us, event | category | flops | bytes accessed | tf_op | source)
XLA Modules:
  0.0 233.8 jit_solution(14968042142638872204)
XLA Ops:
  8.1 180.8 %while.21 = (s32[]{:T(128)}, bf16[64,2048]{1,0:T(8,128)(2,1)S(1)}, bf16[8,64,2048]{2,1,0:T(8,128)(2,1)S(1)}, f32[60]{0:T(128)S(1)}, f32[60]{0:T(128)S(1)}, /*ind...) while((s32[]{:T(128)}, bf16[64,2048]{1,0:T(8,128)(2,1)S(1)}, ...), condition=%wide.region_6.7_spmd.clone, body=%wide.region_0.6_spmd.clone.sunk | while | flops 570639360 | bytes 13007534 | solution.py:74
  10.6 1.3 fusion.34
  12.0 5.2 %bitcast_dynamic-update-slice_fusion.2 = (bf16[8,64,2048]{2,1,0:T(8,128)(2,1)S(1)}, bf16[64,2048]{1,0:T(8,128)(2,1)S(1)}) fusion(bf16[8,64,2048]{2,1,0:T(8,128)(2,1)S(1)} %get-tuple-element.472, s32[]{:T(128)S(6)} %min.11, bf16[1,64,2048]{2,1,0:T(8,128)(2,1)S(1)} %constant_dynamic-slice_fusion.2, pred[]{:T(512)S(6)} %and.22, ...), kind=kOutput, calls=%fused_computation.12.clone.1 | convolution fusion | flops 553790720 | bytes 10036229 | tf_op jit(solution)/shard_map/while/body/eval_jaxpr/dot_general | solution.py:27
  17.2 1.3 collective-permute-start
  18.6 2.2 collective-permute-done
  23.4 1.3 fusion.34
  24.7 5.2 %bitcast_dynamic-update-slice_fusion.2 = (bf16[8,64,2048]{2,1,0:T(8,128)(2,1)S(1)}, bf16[64,2048]{1,0:T(8,128)(2,1)S(1)}) fusion(bf16[8,64,2048]{2,1,0:T(8,128)(2,1)S(1)} %get-tuple-element.472, s32[]{:T(128)S(6)} %min.11, bf16[1,64,2048]{2,1,0:T(8,128)(2,1)S(1)} %constant_dynamic-slice_fusion.2, pred[]{:T(512)S(6)} %and.22, ...), kind=kOutput, calls=%fused_computation.12.clone.1 | convolution fusion | flops 553790720 | bytes 10036229 | tf_op jit(solution)/shard_map/while/body/eval_jaxpr/dot_general | solution.py:27
  30.0 1.3 collective-permute-start
  31.4 6.3 %collective-permute-done = bf16[64,2048]{1,0:T(8,128)(2,1)S(1)} collective-permute-done((bf16[64,2048]{1,0:T(8,128)(2,1)S(1)}, bf16[64,2048]{1,0:T(8,128)(2,1)S(1)}, u32[]{:S(2)}, u32[]{:S(2)}) %collective-permute-start) | collective-permute-done | bytes 262176 | tf_op jit(solution)/shard_map/while/body/eval_jaxpr/ppermute | solution.py:10
  40.2 1.4 fusion.34
  41.5 5.2 %bitcast_dynamic-update-slice_fusion.2 = (bf16[8,64,2048]{2,1,0:T(8,128)(2,1)S(1)}, bf16[64,2048]{1,0:T(8,128)(2,1)S(1)}) fusion(bf16[8,64,2048]{2,1,0:T(8,128)(2,1)S(1)} %get-tuple-element.472, s32[]{:T(128)S(6)} %min.11, bf16[1,64,2048]{2,1,0:T(8,128)(2,1)S(1)} %constant_dynamic-slice_fusion.2, pred[]{:T(512)S(6)} %and.22, ...), kind=kOutput, calls=%fused_computation.12.clone.1 | convolution fusion | flops 553790720 | bytes 10036229 | tf_op jit(solution)/shard_map/while/body/eval_jaxpr/dot_general | solution.py:27
  46.8 1.3 collective-permute-start
  48.2 6.3 %collective-permute-done = bf16[64,2048]{1,0:T(8,128)(2,1)S(1)} collective-permute-done((bf16[64,2048]{1,0:T(8,128)(2,1)S(1)}, bf16[64,2048]{1,0:T(8,128)(2,1)S(1)}, u32[]{:S(2)}, u32[]{:S(2)}) %collective-permute-start) | collective-permute-done | bytes 262176 | tf_op jit(solution)/shard_map/while/body/eval_jaxpr/ppermute | solution.py:10
  57.0 1.3 fusion.34
  58.3 5.2 %bitcast_dynamic-update-slice_fusion.2 = (bf16[8,64,2048]{2,1,0:T(8,128)(2,1)S(1)}, bf16[64,2048]{1,0:T(8,128)(2,1)S(1)}) fusion(bf16[8,64,2048]{2,1,0:T(8,128)(2,1)S(1)} %get-tuple-element.472, s32[]{:T(128)S(6)} %min.11, bf16[1,64,2048]{2,1,0:T(8,128)(2,1)S(1)} %constant_dynamic-slice_fusion.2, pred[]{:T(512)S(6)} %and.22, ...), kind=kOutput, calls=%fused_computation.12.clone.1 | convolution fusion | flops 553790720 | bytes 10036229 | tf_op jit(solution)/shard_map/while/body/eval_jaxpr/dot_general | solution.py:27
  63.6 1.3 collective-permute-start
  65.0 6.3 %collective-permute-done = bf16[64,2048]{1,0:T(8,128)(2,1)S(1)} collective-permute-done((bf16[64,2048]{1,0:T(8,128)(2,1)S(1)}, bf16[64,2048]{1,0:T(8,128)(2,1)S(1)}, u32[]{:S(2)}, u32[]{:S(2)}) %collective-permute-start) | collective-permute-done | bytes 262176 | tf_op jit(solution)/shard_map/while/body/eval_jaxpr/ppermute | solution.py:10
  73.8 1.4 fusion.34
  75.1 5.2 %bitcast_dynamic-update-slice_fusion.2 = (bf16[8,64,2048]{2,1,0:T(8,128)(2,1)S(1)}, bf16[64,2048]{1,0:T(8,128)(2,1)S(1)}) fusion(bf16[8,64,2048]{2,1,0:T(8,128)(2,1)S(1)} %get-tuple-element.472, s32[]{:T(128)S(6)} %min.11, bf16[1,64,2048]{2,1,0:T(8,128)(2,1)S(1)} %constant_dynamic-slice_fusion.2, pred[]{:T(512)S(6)} %and.22, ...), kind=kOutput, calls=%fused_computation.12.clone.1 | convolution fusion | flops 553790720 | bytes 10036229 | tf_op jit(solution)/shard_map/while/body/eval_jaxpr/dot_general | solution.py:27
  80.4 1.3 collective-permute-start
  81.8 6.3 %collective-permute-done = bf16[64,2048]{1,0:T(8,128)(2,1)S(1)} collective-permute-done((bf16[64,2048]{1,0:T(8,128)(2,1)S(1)}, bf16[64,2048]{1,0:T(8,128)(2,1)S(1)}, u32[]{:S(2)}, u32[]{:S(2)}) %collective-permute-start) | collective-permute-done | bytes 262176 | tf_op jit(solution)/shard_map/while/body/eval_jaxpr/ppermute | solution.py:10
  90.6 1.3 fusion.34
  91.9 5.2 %bitcast_dynamic-update-slice_fusion.2 = (bf16[8,64,2048]{2,1,0:T(8,128)(2,1)S(1)}, bf16[64,2048]{1,0:T(8,128)(2,1)S(1)}) fusion(bf16[8,64,2048]{2,1,0:T(8,128)(2,1)S(1)} %get-tuple-element.472, s32[]{:T(128)S(6)} %min.11, bf16[1,64,2048]{2,1,0:T(8,128)(2,1)S(1)} %constant_dynamic-slice_fusion.2, pred[]{:T(512)S(6)} %and.22, ...), kind=kOutput, calls=%fused_computation.12.clone.1 | convolution fusion | flops 553790720 | bytes 10036229 | tf_op jit(solution)/shard_map/while/body/eval_jaxpr/dot_general | solution.py:27
  97.2 1.3 collective-permute-start
  98.6 6.3 %collective-permute-done = bf16[64,2048]{1,0:T(8,128)(2,1)S(1)} collective-permute-done((bf16[64,2048]{1,0:T(8,128)(2,1)S(1)}, bf16[64,2048]{1,0:T(8,128)(2,1)S(1)}, u32[]{:S(2)}, u32[]{:S(2)}) %collective-permute-start) | collective-permute-done | bytes 262176 | tf_op jit(solution)/shard_map/while/body/eval_jaxpr/ppermute | solution.py:10
  107.4 1.4 fusion.34
  108.7 5.2 %bitcast_dynamic-update-slice_fusion.2 = (bf16[8,64,2048]{2,1,0:T(8,128)(2,1)S(1)}, bf16[64,2048]{1,0:T(8,128)(2,1)S(1)}) fusion(bf16[8,64,2048]{2,1,0:T(8,128)(2,1)S(1)} %get-tuple-element.472, s32[]{:T(128)S(6)} %min.11, bf16[1,64,2048]{2,1,0:T(8,128)(2,1)S(1)} %constant_dynamic-slice_fusion.2, pred[]{:T(512)S(6)} %and.22, ...), kind=kOutput, calls=%fused_computation.12.clone.1 | convolution fusion | flops 553790720 | bytes 10036229 | tf_op jit(solution)/shard_map/while/body/eval_jaxpr/dot_general | solution.py:27
  114.0 1.3 collective-permute-start
  115.4 6.3 %collective-permute-done = bf16[64,2048]{1,0:T(8,128)(2,1)S(1)} collective-permute-done((bf16[64,2048]{1,0:T(8,128)(2,1)S(1)}, bf16[64,2048]{1,0:T(8,128)(2,1)S(1)}, u32[]{:S(2)}, u32[]{:S(2)}) %collective-permute-start) | collective-permute-done | bytes 262176 | tf_op jit(solution)/shard_map/while/body/eval_jaxpr/ppermute | solution.py:10
  124.2 1.3 fusion.34
  125.5 5.2 %bitcast_dynamic-update-slice_fusion.2 = (bf16[8,64,2048]{2,1,0:T(8,128)(2,1)S(1)}, bf16[64,2048]{1,0:T(8,128)(2,1)S(1)}) fusion(bf16[8,64,2048]{2,1,0:T(8,128)(2,1)S(1)} %get-tuple-element.472, s32[]{:T(128)S(6)} %min.11, bf16[1,64,2048]{2,1,0:T(8,128)(2,1)S(1)} %constant_dynamic-slice_fusion.2, pred[]{:T(512)S(6)} %and.22, ...), kind=kOutput, calls=%fused_computation.12.clone.1 | convolution fusion | flops 553790720 | bytes 10036229 | tf_op jit(solution)/shard_map/while/body/eval_jaxpr/dot_general | solution.py:27
  130.8 1.3 collective-permute-start
  132.2 6.3 %collective-permute-done = bf16[64,2048]{1,0:T(8,128)(2,1)S(1)} collective-permute-done((bf16[64,2048]{1,0:T(8,128)(2,1)S(1)}, bf16[64,2048]{1,0:T(8,128)(2,1)S(1)}, u32[]{:S(2)}, u32[]{:S(2)}) %collective-permute-start) | collective-permute-done | bytes 262176 | tf_op jit(solution)/shard_map/while/body/eval_jaxpr/ppermute | solution.py:10
  141.0 1.4 fusion.34
  142.4 5.2 %bitcast_dynamic-update-slice_fusion.2 = (bf16[8,64,2048]{2,1,0:T(8,128)(2,1)S(1)}, bf16[64,2048]{1,0:T(8,128)(2,1)S(1)}) fusion(bf16[8,64,2048]{2,1,0:T(8,128)(2,1)S(1)} %get-tuple-element.472, s32[]{:T(128)S(6)} %min.11, bf16[1,64,2048]{2,1,0:T(8,128)(2,1)S(1)} %constant_dynamic-slice_fusion.2, pred[]{:T(512)S(6)} %and.22, ...), kind=kOutput, calls=%fused_computation.12.clone.1 | convolution fusion | flops 553790720 | bytes 10036229 | tf_op jit(solution)/shard_map/while/body/eval_jaxpr/dot_general | solution.py:27
  147.6 1.3 collective-permute-start
  149.0 6.3 %collective-permute-done = bf16[64,2048]{1,0:T(8,128)(2,1)S(1)} collective-permute-done((bf16[64,2048]{1,0:T(8,128)(2,1)S(1)}, bf16[64,2048]{1,0:T(8,128)(2,1)S(1)}, u32[]{:S(2)}, u32[]{:S(2)}) %collective-permute-start) | collective-permute-done | bytes 262176 | tf_op jit(solution)/shard_map/while/body/eval_jaxpr/ppermute | solution.py:10
  157.8 1.3 fusion.34
  159.1 5.2 %bitcast_dynamic-update-slice_fusion.2 = (bf16[8,64,2048]{2,1,0:T(8,128)(2,1)S(1)}, bf16[64,2048]{1,0:T(8,128)(2,1)S(1)}) fusion(bf16[8,64,2048]{2,1,0:T(8,128)(2,1)S(1)} %get-tuple-element.472, s32[]{:T(128)S(6)} %min.11, bf16[1,64,2048]{2,1,0:T(8,128)(2,1)S(1)} %constant_dynamic-slice_fusion.2, pred[]{:T(512)S(6)} %and.22, ...), kind=kOutput, calls=%fused_computation.12.clone.1 | convolution fusion | flops 553790720 | bytes 10036229 | tf_op jit(solution)/shard_map/while/body/eval_jaxpr/dot_general | solution.py:27
  164.4 1.3 collective-permute-start
  165.8 6.3 %collective-permute-done = bf16[64,2048]{1,0:T(8,128)(2,1)S(1)} collective-permute-done((bf16[64,2048]{1,0:T(8,128)(2,1)S(1)}, bf16[64,2048]{1,0:T(8,128)(2,1)S(1)}, u32[]{:S(2)}, u32[]{:S(2)}) %collective-permute-start) | collective-permute-done | bytes 262176 | tf_op jit(solution)/shard_map/while/body/eval_jaxpr/ppermute | solution.py:10
  174.6 1.4 fusion.34
  176.0 5.2 %bitcast_dynamic-update-slice_fusion.2 = (bf16[8,64,2048]{2,1,0:T(8,128)(2,1)S(1)}, bf16[64,2048]{1,0:T(8,128)(2,1)S(1)}) fusion(bf16[8,64,2048]{2,1,0:T(8,128)(2,1)S(1)} %get-tuple-element.472, s32[]{:T(128)S(6)} %min.11, bf16[1,64,2048]{2,1,0:T(8,128)(2,1)S(1)} %constant_dynamic-slice_fusion.2, pred[]{:T(512)S(6)} %and.22, ...), kind=kOutput, calls=%fused_computation.12.clone.1 | convolution fusion | flops 553790720 | bytes 10036229 | tf_op jit(solution)/shard_map/while/body/eval_jaxpr/dot_general | solution.py:27
  181.2 1.3 collective-permute-start
  182.6 6.3 %collective-permute-done = bf16[64,2048]{1,0:T(8,128)(2,1)S(1)} collective-permute-done((bf16[64,2048]{1,0:T(8,128)(2,1)S(1)}, bf16[64,2048]{1,0:T(8,128)(2,1)S(1)}, u32[]{:S(2)}, u32[]{:S(2)}) %collective-permute-start) | collective-permute-done | bytes 262176 | tf_op jit(solution)/shard_map/while/body/eval_jaxpr/ppermute | solution.py:10
  188.9 1.3 copy-done
  190.3 18.2 %all-reduce = (f32[60]{0:T(128)S(1)}, f32[60]{0:T(128)S(1)}) all-reduce(f32[60]{0:T(128)S(1)} %get-tuple-element.261, f32[60]{0:T(128)S(1)} %get-tuple-element.260), channel_id=1, replica_groups=mesh['section'=4,'dp'=8] {'dp'}, use_global_device_ids=true, to_apply=%region_9.10 | all-reduce | flops 120 | bytes 960 | tf_op jit(solution)/shard_map/psum | solution.py:75
  209.7 16.1 %reduce-scatter.2.cloned.1.call-done = bf16[2,64,2048]{2,1,0:T(8,128)(2,1)} async-done(((bf16[8,64,2048]{2,1,0:T(8,128)(2,1)}), bf16[2,64,2048]{2,1,0:T(8,128)(2,1)}) %reduce-scatter.2.cloned.1.call-update) | async-done | bytes 524304 | tf_op jit(solution)/shard_map/reduce_scatter | solution.py:82
  (111 shorter events, 30.1 us)
Async XLA Ops:
  7.2 1.0 copy-start.1
  7.2 0.9 copy-start.2
  7.2 218.6 %reduce-scatter.2.cloned.1.call-start = ((), (), s32[]{:S(2)}) async-start(), calls=%async_computation.1 | async-start | bytes 2621440 | tf_op jit(solution)/shard_map/reduce_scatter | solution.py:82
  17.2 3.6 %collective-permute-start = (bf16[64,2048]{1,0:T(8,128)(2,1)S(1)}, bf16[64,2048]{1,0:T(8,128)(2,1)S(1)}, u32[]{:S(2)}, u32[]{:S(2)}) collective-permute-start(bf16[64,2048]{1,0:T(8,128)(2,1)S(1)} %get-tuple-element.447), channel_id=1, source_target_pairs={{0,8},{8,16},{16,24},{1,9},{9,17},{17,25},{2,10},{10,18},{18,26},{... | collective-permute-start | bytes 786440 | tf_op jit(solution)/shard_map/while/body/eval_jaxpr/ppermute | solution.py:10
  30.0 7.7 %collective-permute-start = (bf16[64,2048]{1,0:T(8,128)(2,1)S(1)}, bf16[64,2048]{1,0:T(8,128)(2,1)S(1)}, u32[]{:S(2)}, u32[]{:S(2)}) collective-permute-start(bf16[64,2048]{1,0:T(8,128)(2,1)S(1)} %get-tuple-element.447), channel_id=1, source_target_pairs={{0,8},{8,16},{16,24},{1,9},{9,17},{17,25},{2,10},{10,18},{18,26},{... | collective-permute-start | bytes 786440 | tf_op jit(solution)/shard_map/while/body/eval_jaxpr/ppermute | solution.py:10
  46.8 7.7 %collective-permute-start = (bf16[64,2048]{1,0:T(8,128)(2,1)S(1)}, bf16[64,2048]{1,0:T(8,128)(2,1)S(1)}, u32[]{:S(2)}, u32[]{:S(2)}) collective-permute-start(bf16[64,2048]{1,0:T(8,128)(2,1)S(1)} %get-tuple-element.447), channel_id=1, source_target_pairs={{0,8},{8,16},{16,24},{1,9},{9,17},{17,25},{2,10},{10,18},{18,26},{... | collective-permute-start | bytes 786440 | tf_op jit(solution)/shard_map/while/body/eval_jaxpr/ppermute | solution.py:10
  63.6 7.7 %collective-permute-start = (bf16[64,2048]{1,0:T(8,128)(2,1)S(1)}, bf16[64,2048]{1,0:T(8,128)(2,1)S(1)}, u32[]{:S(2)}, u32[]{:S(2)}) collective-permute-start(bf16[64,2048]{1,0:T(8,128)(2,1)S(1)} %get-tuple-element.447), channel_id=1, source_target_pairs={{0,8},{8,16},{16,24},{1,9},{9,17},{17,25},{2,10},{10,18},{18,26},{... | collective-permute-start | bytes 786440 | tf_op jit(solution)/shard_map/while/body/eval_jaxpr/ppermute | solution.py:10
  80.4 7.7 %collective-permute-start = (bf16[64,2048]{1,0:T(8,128)(2,1)S(1)}, bf16[64,2048]{1,0:T(8,128)(2,1)S(1)}, u32[]{:S(2)}, u32[]{:S(2)}) collective-permute-start(bf16[64,2048]{1,0:T(8,128)(2,1)S(1)} %get-tuple-element.447), channel_id=1, source_target_pairs={{0,8},{8,16},{16,24},{1,9},{9,17},{17,25},{2,10},{10,18},{18,26},{... | collective-permute-start | bytes 786440 | tf_op jit(solution)/shard_map/while/body/eval_jaxpr/ppermute | solution.py:10
  97.2 7.7 %collective-permute-start = (bf16[64,2048]{1,0:T(8,128)(2,1)S(1)}, bf16[64,2048]{1,0:T(8,128)(2,1)S(1)}, u32[]{:S(2)}, u32[]{:S(2)}) collective-permute-start(bf16[64,2048]{1,0:T(8,128)(2,1)S(1)} %get-tuple-element.447), channel_id=1, source_target_pairs={{0,8},{8,16},{16,24},{1,9},{9,17},{17,25},{2,10},{10,18},{18,26},{... | collective-permute-start | bytes 786440 | tf_op jit(solution)/shard_map/while/body/eval_jaxpr/ppermute | solution.py:10
  114.0 7.7 %collective-permute-start = (bf16[64,2048]{1,0:T(8,128)(2,1)S(1)}, bf16[64,2048]{1,0:T(8,128)(2,1)S(1)}, u32[]{:S(2)}, u32[]{:S(2)}) collective-permute-start(bf16[64,2048]{1,0:T(8,128)(2,1)S(1)} %get-tuple-element.447), channel_id=1, source_target_pairs={{0,8},{8,16},{16,24},{1,9},{9,17},{17,25},{2,10},{10,18},{18,26},{... | collective-permute-start | bytes 786440 | tf_op jit(solution)/shard_map/while/body/eval_jaxpr/ppermute | solution.py:10
  130.8 7.7 %collective-permute-start = (bf16[64,2048]{1,0:T(8,128)(2,1)S(1)}, bf16[64,2048]{1,0:T(8,128)(2,1)S(1)}, u32[]{:S(2)}, u32[]{:S(2)}) collective-permute-start(bf16[64,2048]{1,0:T(8,128)(2,1)S(1)} %get-tuple-element.447), channel_id=1, source_target_pairs={{0,8},{8,16},{16,24},{1,9},{9,17},{17,25},{2,10},{10,18},{18,26},{... | collective-permute-start | bytes 786440 | tf_op jit(solution)/shard_map/while/body/eval_jaxpr/ppermute | solution.py:10
  147.6 7.7 %collective-permute-start = (bf16[64,2048]{1,0:T(8,128)(2,1)S(1)}, bf16[64,2048]{1,0:T(8,128)(2,1)S(1)}, u32[]{:S(2)}, u32[]{:S(2)}) collective-permute-start(bf16[64,2048]{1,0:T(8,128)(2,1)S(1)} %get-tuple-element.447), channel_id=1, source_target_pairs={{0,8},{8,16},{16,24},{1,9},{9,17},{17,25},{2,10},{10,18},{18,26},{... | collective-permute-start | bytes 786440 | tf_op jit(solution)/shard_map/while/body/eval_jaxpr/ppermute | solution.py:10
  164.4 7.7 %collective-permute-start = (bf16[64,2048]{1,0:T(8,128)(2,1)S(1)}, bf16[64,2048]{1,0:T(8,128)(2,1)S(1)}, u32[]{:S(2)}, u32[]{:S(2)}) collective-permute-start(bf16[64,2048]{1,0:T(8,128)(2,1)S(1)} %get-tuple-element.447), channel_id=1, source_target_pairs={{0,8},{8,16},{16,24},{1,9},{9,17},{17,25},{2,10},{10,18},{18,26},{... | collective-permute-start | bytes 786440 | tf_op jit(solution)/shard_map/while/body/eval_jaxpr/ppermute | solution.py:10
  181.2 7.7 %collective-permute-start = (bf16[64,2048]{1,0:T(8,128)(2,1)S(1)}, bf16[64,2048]{1,0:T(8,128)(2,1)S(1)}, u32[]{:S(2)}, u32[]{:S(2)}) collective-permute-start(bf16[64,2048]{1,0:T(8,128)(2,1)S(1)} %get-tuple-element.447), channel_id=1, source_target_pairs={{0,8},{8,16},{16,24},{1,9},{9,17},{17,25},{2,10},{10,18},{18,26},{... | collective-permute-start | bytes 786440 | tf_op jit(solution)/shard_map/while/body/eval_jaxpr/ppermute | solution.py:10
  188.9 1.4 copy-start
Sparse Core Ops, SparseCore 0:
  190.4 35.3 reduce-scatter.1
where the time goes:
time: 238 us; the launch traced here: 234 us
  waiting for transfers between devices  81 us (34%)
  matrix products  72.5 us (30%)
  other arithmetic  20.5 us (9%)
  blocking collectives  18.2 us (8%)
  between operations  15.9 us (7%)
  starting transfers between devices  14.2 us (6%)
  local copies, waits for them, and re-layouts  10.9 us (5%)
    ppermute x11, waiting for transfers between devices, from_behind(): return lax.ppermute(block, axis, route)  64.8 us
    dot_general x11, matrix products, router_layer(): update = jnp.dot(mixed_rows, w_mix, preferred_element_type=jnp.float32)  57.6 us
    psum x1, blocking collectives, per_device(): count_total, prob_total = lax.psum((count_total, prob_total), 'dp')  18.2 us
    reduce_scatter x1, waiting for transfers between devices, per_device(): lax.psum_scatter(terms.astype(jnp.bfloat16), 'section', scatter_dimension...  16.1 us
    dot_general x11, matrix products, router_layer(): jnp.dot(normed.astype(jnp.bfloat16), w_router, preferred_element_type=jnp...  14.9 us
    ppermute x11, starting transfers between devices, from_behind(): return lax.ppermute(block, axis, route)  14.2 us
    reduce_sum x11, other arithmetic, router_layer(): mean_square = jnp.mean(state_wide * state_wide, axis=-1, keepdims=True)  12.6 us
    eq x11, local copies, waits for them, and re-layouts, router_layer(): chosen_ids[:, :, None] == expert_ids[None, None, :]  7.56 us
  transfers between devices with their start and end apart: 12, of which 12 were waited for; matrix products, arithmetic and copies ran while one was open for 1% of the time, Pallas kernels for 0%

commit v1 on v0

v1 whole, which is shorter than its diff:
```python
import functools

import jax
import jax.numpy as jnp
from jax import lax
from jax.experimental import pallas as pl
from jax.experimental.pallas import tpu as pltpu
from jax.sharding import PartitionSpec as P

MESH = pl.DeviceIdType.MESH


def relay(
    sections,
    shards,
    chunk,
    hidden,
    gain,
    router,
    scale,
    mix,
    routes,
    out,
    loss,
    arrived,
    left,
    weights,
    router_v,
    scale_v,
    gain_v,
    routes_v,
    normed_v,
    normed_b,
    mixed_v,
    stats,
    all_stats,
    in_sem,
    send_sem,
    out_sem,
    weight_sem,
    table_sem,
    stat_send,
    stat_recv,
):
    section = lax.axis_index("section")
    shard = lax.axis_index("dp")
    batches, rows, width = arrived.shape
    experts = router_v.shape[1]
    owned = batches // sections
    pieces = width // chunk
    last = sections - 1

    tables = (
        pltpu.make_async_copy(gain, gain_v, table_sem.at[0]),
        pltpu.make_async_copy(router.at[0], router_v, table_sem.at[1]),
        pltpu.make_async_copy(routes.at[0], routes_v, table_sem.at[2]),
        pltpu.make_async_copy(scale.at[0], scale_v, table_sem.at[3]),
    )

    def own_input(batch):
        return pltpu.make_async_copy(hidden.at[batch], arrived.at[batch], in_sem.at[batch])

    def weight_piece(piece):
        columns = pl.ds(piece * chunk, chunk)
        return pltpu.make_async_copy(
            mix.at[0, :, columns], weights.at[:, columns], weight_sem.at[piece]
        )

    @pl.when(section == 0)
    def _():
        own_input(0).start()

    for table in tables:
        table.start()
    for piece in range(pieces):
        weight_piece(piece).start()

    @pl.when(section == 0)
    def _():
        for batch in range(1, batches):
            own_input(batch).start()

    barrier = pltpu.get_barrier_semaphore()
    for step in range(1, sections):
        pl.semaphore_signal(
            barrier,
            inc=1,
            device_id={"section": lax.rem(section + step, sections)},
            device_id_type=MESH,
        )
    for step in range(1, shards):
        pl.semaphore_signal(
            barrier, inc=1, device_id={"dp": lax.rem(shard + step, shards)}, device_id_type=MESH
        )
    stats[...] = jnp.zeros_like(stats)
    for table in tables:
        table.wait()
    pl.semaphore_wait(barrier, sections - 1 + shards - 1)

    def peer_stats(step):
        return pltpu.make_async_remote_copy(
            src_ref=all_stats.at[shard],
            dst_ref=all_stats.at[shard],
            send_sem=stat_send,
            recv_sem=stat_recv,
            device_id={"dp": lax.rem(shard + step, shards)},
            device_id_type=MESH,
        )

    def one_batch(batch, carry):
        own_input(batch).wait()
        square = jnp.zeros((rows, 128), jnp.float32)
        for at in range(0, width, 128):
            part = arrived[batch, :, at : at + 128].astype(jnp.float32)
            square = square + part * part
        mean_square = jnp.sum(square, axis=-1, keepdims=True) / jnp.float32(width)
        inverse = lax.rsqrt(mean_square + 1e-06)
        for at in range(0, width, 256):
            part = arrived[batch, :, at : at + 256].astype(jnp.float32)
            normed = part * inverse * gain_v[:, at : at + 256].astype(jnp.float32)
            normed_v[:, at : at + 256] = normed
            normed_b[:, at : at + 256] = normed.astype(jnp.bfloat16)
        logits = jnp.dot(normed_b[...], router_v[...], preferred_element_type=jnp.float32)
        exponent = jnp.exp(logits)
        probabilities = exponent / jnp.sum(exponent, axis=-1, keepdims=True)
        ids = routes_v[batch]
        lanes = lax.broadcasted_iota(jnp.int32, (rows, experts), 1)
        onehot = jnp.zeros((rows, experts), jnp.float32)
        for pick in range(ids.shape[1]):
            onehot = onehot + (ids[:, pick : pick + 1] == lanes).astype(jnp.float32)
        gates = (probabilities * onehot).astype(jnp.bfloat16)
        stats[0:1, 0:experts] += jnp.sum(onehot, axis=0, keepdims=True)
        stats[1:2, 0:experts] += jnp.sum(probabilities, axis=0, keepdims=True)

        for at in range(0, width, 256):
            channel = jnp.dot(
                gates, scale_v[:, at : at + 256], preferred_element_type=jnp.float32
            )
            mixed_v[:, at : at + 256] = (normed_v[:, at : at + 256] * channel).astype(jnp.bfloat16)

        @pl.when(batch == batches - 1)
        def _():
            all_stats[shard] = stats[...]

        @pl.when(batch == 0)
        def _():
            for piece in range(pieces):
                weight_piece(piece).wait()

        @pl.when(batch == batches - 1)
        def _():
            for step in range(1, shards):
                peer_stats(step).start()

        owner = batch // owned
        for piece in range(pieces):
            at = piece * chunk
            update = jnp.dot(
                mixed_v[...], weights[:, at : at + chunk], preferred_element_type=jnp.float32
            )
            state = arrived[batch, :, at : at + chunk].astype(jnp.float32)
            left[batch, :, at : at + chunk] = (state + update).astype(jnp.bfloat16)

            @pl.when(section < last)
            def _():
                pltpu.make_async_remote_copy(
                    src_ref=left.at[batch, :, pl.ds(at, chunk)],
                    dst_ref=arrived.at[batch, :, pl.ds(at, chunk)],
                    send_sem=send_sem.at[batch],
                    recv_sem=in_sem.at[batch],
                    device_id={"section": section + 1},
                    device_id_type=MESH,
                ).start()

            @pl.when((section == last) & (owner != last))
            def _():
                pltpu.make_async_remote_copy(
                    src_ref=left.at[batch, :, pl.ds(at, chunk)],
                    dst_ref=out.at[lax.rem(batch, owned), :, pl.ds(at, chunk)],
                    send_sem=send_sem.at[batch],
                    recv_sem=out_sem.at[lax.rem(batch, owned)],
                    device_id={"section": owner},
                    device_id_type=MESH,
                ).start()

            @pl.when((section == last) & (owner == last))
            def _():
                pltpu.make_async_copy(
                    left.at[batch, :, pl.ds(at, chunk)],
                    out.at[lax.rem(batch, owned), :, pl.ds(at, chunk)],
                    out_sem.at[lax.rem(batch, owned)],
                ).start()

        return carry

    lax.fori_loop(0, batches, one_batch, 0)

    for slot in range(owned):
        pltpu.make_async_copy(out.at[slot], out.at[slot], out_sem.at[slot]).wait()
    for batch in range(batches):

        @pl.when((section < last) | (batch // owned != last))
        def _():
            pltpu.make_async_copy(left.at[batch], left.at[batch], send_sem.at[batch]).wait()

    others = all_stats.at[pl.ds(0, shards - 1)]
    pltpu.make_async_copy(others, others, stat_send).wait()
    pltpu.make_async_copy(others, others, stat_recv).wait()
    total = all_stats[0]
    for at in range(1, shards):
        total = total + all_stats[at]
    tokens = jnp.float32(batches * rows * shards)
    fractions = total[0:1, :] / (tokens * jnp.float32(routes_v.shape[2]))
    mean_probs = total[1:2, :] / tokens
    loss[0] = jnp.float32(experts) * jnp.sum(fractions * mean_probs)


def per_device(hidden_in, norm_gain, router_weight, expert_scale, mix_weight, routes):
    sections = lax.axis_size("section")
    shards = lax.axis_size("dp")
    batches, rows, width = hidden_in.shape
    experts = router_weight.shape[2]
    picks = routes.shape[3]
    chunk = 256
    pieces = width // chunk
    anywhere = pl.BlockSpec(memory_space=pl.ANY)
    return pl.pallas_call(
        functools.partial(relay, sections, shards, chunk),
        out_shape=(
            jax.ShapeDtypeStruct((batches // sections, rows, width), jnp.bfloat16),
            jax.ShapeDtypeStruct((1,), jnp.float32),
        ),
        in_specs=[anywhere] * 6,
        out_specs=(anywhere, pl.BlockSpec(memory_space=pltpu.SMEM)),
        scratch_shapes=[
            pltpu.VMEM((batches, rows, width), jnp.bfloat16),
            pltpu.VMEM((batches, rows, width), jnp.bfloat16),
            pltpu.VMEM((width, width), jnp.bfloat16),
            pltpu.VMEM((width, experts), jnp.bfloat16),
            pltpu.VMEM((experts, width), jnp.bfloat16),
            pltpu.VMEM((1, width), jnp.bfloat16),
            pltpu.VMEM((batches, rows, picks), jnp.int32),
            pltpu.VMEM((rows, width), jnp.float32),
            pltpu.VMEM((rows, width), jnp.bfloat16),
            pltpu.VMEM((rows, width), jnp.bfloat16),
            pltpu.VMEM((8, 128), jnp.float32),
            pltpu.VMEM((shards, 8, 128), jnp.float32),
            pltpu.SemaphoreType.DMA((batches,)),
            pltpu.SemaphoreType.DMA((batches,)),
            pltpu.SemaphoreType.DMA((batches // sections,)),
            pltpu.SemaphoreType.DMA((pieces,)),
            pltpu.SemaphoreType.DMA((4,)),
            pltpu.SemaphoreType.DMA,
            pltpu.SemaphoreType.DMA,
        ],
        compiler_params=pltpu.CompilerParams(collective_id=0, has_side_effects=True),
    )(hidden_in, norm_gain, router_weight, expert_scale, mix_weight, routes)


def solution(mesh):
    placed = (
        P(None, "dp", None),
        P("section", None),
        P("section", None, None),
        P("section", None, None),
        P("section", None, None),
        P("section", None, "dp", None),
    )
    return jax.shard_map(
        per_device,
        mesh=mesh,
        in_specs=placed,
        out_specs=(P("section", "dp", None), P("section")),
        check_vma=False,
    )
```

time: 238 us -> 64.8 us (0.27); the launches traced: 234 us -> 64.5 us
  waiting for transfers between devices: 81 us -> 0 us
  matrix products: 72.5 us -> 0 us
  Pallas kernels: 0 us -> 56.8 us
  other arithmetic: 20.5 us -> 0 us
  blocking collectives: 18.2 us -> 0 us
  starting transfers between devices: 14.2 us -> 0 us
  between operations: 15.9 us -> 2.32 us
  local copies, waits for them, and re-layouts: 10.9 us -> 5.43 us
    dot_general x22 -> x0, matrix products: 72.5 us -> none  [the longest x11 57.6 us: router_layer(): update = jnp.dot(mixed_rows, w_mix, preferred_element_type=jnp.float32)]
    ppermute x11 -> x0, waiting for transfers between devices: 64.8 us -> none  [from_behind(): return lax.ppermute(block, axis, route)]
    pallas_call x0 -> x1, Pallas kernels: none -> 56.8 us  [per_device(): pl.pallas_call(functools.partial(relay, sections, shards, chunk), out_sha...]
    reduce_sum x34 -> x0, other arithmetic: 20.2 us -> none  [the longest x11 12.6 us: router_layer(): mean_square = jnp.mean(state_wide * state_wide, axis=-1, keepdims=True)]
    psum x1 -> x0, blocking collectives: 18.2 us -> none  [per_device(): count_total, prob_total = lax.psum((count_total, prob_total), 'dp')]
    reduce_scatter x1 -> x0, waiting for transfers between devices: 16.1 us -> none  [per_device(): lax.psum_scatter(terms.astype(jnp.bfloat16), 'section', scatter_dimension...]
    ppermute x11 -> x0, starting transfers between devices: 14.2 us -> none  [from_behind(): return lax.ppermute(block, axis, route)]
    eq x11 -> x0, local copies, waits for them, and re-layouts: 7.56 us -> none  [router_layer(): chosen_ids[:, :, None] == expert_ids[None, None, :]]
  transfers between devices with their start and end apart: 12 -> 0, of which waited for: 12 -> 0; matrix products, arithmetic and copies ran while one was open for 1% -> 0% of each run, Pallas kernels for 0% -> 0%
where the time goes in v1:
time: 64.8 us; the launch traced here: 64.5 us
  Pallas kernels  56.8 us (88%)
  local copies, waits for them, and re-layouts  5.43 us (8%)
  between operations  2.32 us (4%)
    pallas_call x1, Pallas kernels, per_device(): pl.pallas_call(functools.partial(relay, sections, shards, chunk), out_sha...  56.8 us
    unnamed x3, local copies, waits for them, and re-layouts  5.43 us

profile of v1, /device:TPU:3, one launch (start us, length us, event | category | flops | bytes accessed | tf_op | source)
XLA Modules:
  0.0 64.5 jit_solution(16774039872608956062)
XLA Ops:
  0.6 1.6 %copy.9.routes = s32[1,8,64,4]{3,2,1,0:T(8,128)} copy(s32[1,8,64,4]{2,3,1,0:T(4,128)} %param.11) | data formatting | bytes 16384 | tf_op args[5]
  2.2 2.0 %copy.8.router = bf16[1,2048,60]{2,1,0:T(8,128)(2,1)} copy(bf16[1,2048,60]{1,2,0:T(8,128)(2,1)} %param.8) | data formatting | bytes 491520 | tf_op args[2]
  4.2 56.8 %shard_map.77 = (bf16[2,64,2048]{2,1,0:T(8,128)(2,1)}, f32[1]{0:T(128)}) custom-call(bf16[8,64,2048]{2,1,0:T(8,128)(2,1)} %hidden.1, bf16[1,2048]{1,0:T(2,128)(2,1)} %gain.1, bf16[1,2048,60]{2,1,0:T(8,128)(2,1)} %copy.8.router, bf16[1,60,2048]{2,1,0:T(8,128)(2,1)} %scale.1, bf16[1,2048,2048]{2,1,0:T(8,128)(2,1)} %mix.1, s32[1,8,64,4]{3,2,1,0:T(8,128)} %copy.9.routes), custom_call_target="tpu_custom_call" | custom-call | tf_op jit(solution)/shard_map/pallas_call | solution.py:227
  61.0 1.9 %copy.12 = bf16[2,64,2048]{2,1,0:T(8,128)(2,1)} copy(bf16[2,64,2048]{2,1,0:T(8,128)(2,1)} %get-tuple-element.4) | data formatting | bytes 1048576

commit v2 on v1

v2 whole, which is shorter than its diff:
```python
import functools

import jax
import jax.numpy as jnp
from jax import lax
from jax.experimental import pallas as pl
from jax.experimental.pallas import tpu as pltpu
from jax.sharding import PartitionSpec as P

MESH = pl.DeviceIdType.MESH


def relay(
    sections,
    shards,
    chunk,
    group,
    hidden,
    gain,
    router,
    scale,
    mix,
    routes,
    out,
    loss,
    arrived,
    left,
    weights,
    router_v,
    scale_v,
    gain_v,
    routes_v,
    normed_v,
    normed_b,
    mixed_v,
    stats,
    all_stats,
    in_sem,
    send_sem,
    out_sem,
    weight_sem,
    table_sem,
    stat_send,
    stat_recv,
):
    section = lax.axis_index("section")
    shard = lax.axis_index("dp")
    batches, rows, width = hidden.shape
    experts, picks = router_v.shape[0], routes_v.shape[1]
    groups, tall = batches // group, group * rows
    owned = batches // sections
    pieces = width // chunk
    last = sections - 1

    tables = (
        pltpu.make_async_copy(gain, gain_v, table_sem.at[0]),
        pltpu.make_async_copy(router, router_v, table_sem.at[1]),
        pltpu.make_async_copy(routes.at[0], routes_v, table_sem.at[2]),
        pltpu.make_async_copy(scale.at[0], scale_v, table_sem.at[3]),
    )

    def own_input(batch):
        place = arrived.at[batch // group, pl.ds(batch % group * rows, rows), :]
        return pltpu.make_async_copy(hidden.at[batch], place, in_sem.at[batch // group])

    def weight_piece(piece):
        columns = pl.ds(piece * chunk, chunk)
        return pltpu.make_async_copy(
            mix.at[0, :, columns], weights.at[:, columns], weight_sem.at[piece]
        )

    @pl.when(section == 0)
    def _():
        for batch in range(group):
            own_input(batch).start()

    for table in tables:
        table.start()
    for piece in range(pieces):
        weight_piece(piece).start()

    @pl.when(section == 0)
    def _():
        for batch in range(group, batches):
            own_input(batch).start()

    barrier = pltpu.get_barrier_semaphore()
    for step in range(1, sections):
        pl.semaphore_signal(
            barrier,
            inc=1,
            device_id={"section": lax.rem(section + step, sections)},
            device_id_type=MESH,
        )
    for step in range(1, shards):
        pl.semaphore_signal(
            barrier, inc=1, device_id={"dp": lax.rem(shard + step, shards)}, device_id_type=MESH
        )
    stats[...] = jnp.zeros_like(stats)
    for table in tables:
        table.wait()

    def peer_stats(step):
        return pltpu.make_async_remote_copy(
            src_ref=all_stats.at[shard],
            dst_ref=all_stats.at[shard],
            send_sem=stat_send,
            recv_sem=stat_recv,
            device_id={"dp": lax.rem(shard + step, shards)},
            device_id_type=MESH,
        )

    def one_group(at_group, carry):
        ids = jnp.concatenate([routes_v[at_group * group + k] for k in range(group)], axis=1)
        sublanes = lax.broadcasted_iota(jnp.int32, (128, tall), 0)
        standing = jnp.zeros((128, tall), jnp.float32)
        for pick in range(picks):
            standing = standing + (ids[pick : pick + 1, :] == sublanes).astype(jnp.float32)
        onehot = jnp.transpose(standing)[:, 0:experts]
        pltpu.make_async_copy(
            arrived.at[at_group], arrived.at[at_group], in_sem.at[at_group]
        ).wait()
        square = jnp.zeros((tall, 128), jnp.float32)
        for at in range(0, width, 128):
            part = arrived[at_group, :, at : at + 128].astype(jnp.float32)
            square = square + part * part
        mean_square = jnp.sum(square, axis=-1, keepdims=True) / jnp.float32(width)
        inverse = lax.rsqrt(mean_square + 1e-06)
        for at in range(0, width, 256):
            part = arrived[at_group, :, at : at + 256].astype(jnp.float32)
            normed = part * inverse * gain_v[:, at : at + 256].astype(jnp.float32)
            normed_v[:, at : at + 256] = normed
            normed_b[:, at : at + 256] = normed.astype(jnp.bfloat16)
        logits = lax.dot_general(
            normed_b[...],
            router_v[...],
            (((1,), (1,)), ((), ())),
            preferred_element_type=jnp.float32,
        )
        exponent = jnp.exp(logits)
        probabilities = exponent / jnp.sum(exponent, axis=-1, keepdims=True)
        gates = (probabilities * onehot).astype(jnp.bfloat16)
        stats[0:1, 0:experts] += jnp.sum(onehot, axis=0, keepdims=True)
        stats[1:2, 0:experts] += jnp.sum(probabilities, axis=0, keepdims=True)

        for at in range(0, width, 256):
            channel = jnp.dot(
                gates, scale_v[:, at : at + 256], preferred_element_type=jnp.float32
            )
            mixed_v[:, at : at + 256] = (normed_v[:, at : at + 256] * channel).astype(jnp.bfloat16)

        @pl.when(at_group == groups - 1)
        def _():
            all_stats[shard] = stats[...]

        @pl.when(at_group == 0)
        def _():
            pl.semaphore_wait(barrier, sections - 1 + shards - 1)

        @pl.when(at_group == groups - 1)
        def _():
            for step in range(1, shards):
                peer_stats(step).start()

        for piece in range(pieces):
            at = piece * chunk
            columns = pl.ds(at, chunk)

            @pl.when(at_group == 0)
            def _():
                weight_piece(piece).wait()

            update = jnp.dot(
                mixed_v[...], weights[:, at : at + chunk], preferred_element_type=jnp.float32
            )
            state = arrived[at_group, :, at : at + chunk].astype(jnp.float32)
            left[at_group, :, at : at + chunk] = (state + update).astype(jnp.bfloat16)

            @pl.when(section < last)
            def _():
                pltpu.make_async_remote_copy(
                    src_ref=left.at[at_group, :, columns],
                    dst_ref=arrived.at[at_group, :, columns],
                    send_sem=send_sem.at[at_group],
                    recv_sem=in_sem.at[at_group],
                    device_id={"section": section + 1},
                    device_id_type=MESH,
                ).start()

            for k in range(group):
                batch = at_group * group + k
                owner = batch // owned

                @pl.when((section == last) & (owner != last))
                def _():
                    pltpu.make_async_remote_copy(
                        src_ref=left.at[at_group, pl.ds(k * rows, rows), columns],
                        dst_ref=out.at[lax.rem(batch, owned), :, columns],
                        send_sem=send_sem.at[at_group],
                        recv_sem=out_sem.at[lax.rem(batch, owned)],
                        device_id={"section": owner},
                        device_id_type=MESH,
                    ).start()

        return carry

    lax.fori_loop(0, groups, one_group, 0)

    @pl.when(section == last)
    def _():
        for slot in range(owned):
            batch = batches - owned + slot
            out[slot] = left[batch // group, pl.ds(batch % group * rows, rows), :]

    @pl.when(section != last)
    def _():
        for slot in range(owned):
            pltpu.make_async_copy(out.at[slot], out.at[slot], out_sem.at[slot]).wait()

    for batch in range(batches):
        sent = left.at[batch // group, pl.ds(batch % group * rows, rows), :]

        @pl.when((section < last) | (batch // owned != last))
        def _():
            pltpu.make_async_copy(sent, sent, send_sem.at[batch // group]).wait()

    others = all_stats.at[pl.ds(0, shards - 1)]
    pltpu.make_async_copy(others, others, stat_send).wait()
    pltpu.make_async_copy(others, others, stat_recv).wait()
    total = all_stats[0]
    for at in range(1, shards):
        total = total + all_stats[at]
    tokens = jnp.float32(batches * rows * shards)
    fractions = total[0:1, :] / (tokens * jnp.float32(picks))
    mean_probs = total[1:2, :] / tokens
    loss[0] = jnp.float32(experts) * jnp.sum(fractions * mean_probs)


def per_device(hidden_in, norm_gain, router_weight, expert_scale, mix_weight, routes):
    sections = lax.axis_size("section")
    shards = lax.axis_size("dp")
    batches, rows, width = hidden_in.shape
    experts = router_weight.shape[2]
    picks = routes.shape[3]
    group = 2 if batches % 2 == 0 else 1
    groups, tall = batches // group, group * rows
    chunk = 256
    pieces = width // chunk
    anywhere = pl.BlockSpec(memory_space=pl.ANY)
    return pl.pallas_call(
        functools.partial(relay, sections, shards, chunk, group),
        out_shape=(
            jax.ShapeDtypeStruct((batches // sections, rows, width), jnp.bfloat16),
            jax.ShapeDtypeStruct((1,), jnp.float32),
        ),
        in_specs=[anywhere] * 6,
        out_specs=(pl.BlockSpec(memory_space=pltpu.VMEM), pl.BlockSpec(memory_space=pltpu.SMEM)),
        scratch_shapes=[
            pltpu.VMEM((groups, tall, width), jnp.bfloat16),
            pltpu.VMEM((groups, tall, width), jnp.bfloat16),
            pltpu.VMEM((width, width), jnp.bfloat16),
            pltpu.VMEM((experts, width), jnp.bfloat16),
            pltpu.VMEM((experts, width), jnp.bfloat16),
            pltpu.VMEM((1, width), jnp.bfloat16),
            pltpu.VMEM((batches, picks, rows), jnp.int32),
            pltpu.VMEM((tall, width), jnp.float32),
            pltpu.VMEM((tall, width), jnp.bfloat16),
            pltpu.VMEM((tall, width), jnp.bfloat16),
            pltpu.VMEM((8, 128), jnp.float32),
            pltpu.VMEM((shards, 8, 128), jnp.float32),
            pltpu.SemaphoreType.DMA((groups,)),
            pltpu.SemaphoreType.DMA((groups,)),
            pltpu.SemaphoreType.DMA((batches // sections,)),
            pltpu.SemaphoreType.DMA((pieces,)),
            pltpu.SemaphoreType.DMA((4,)),
            pltpu.SemaphoreType.DMA,
            pltpu.SemaphoreType.DMA,
        ],
        compiler_params=pltpu.CompilerParams(collective_id=0, has_side_effects=True),
    )(
        hidden_in,
        norm_gain,
        jnp.transpose(router_weight[0]),
        expert_scale,
        mix_weight,
        jnp.swapaxes(routes, 2, 3),
    )


def solution(mesh):
    placed = (
        P(None, "dp", None),
        P("section", None),
        P("section", None, None),
        P("section", None, None),
        P("section", None, None),
        P("section", None, "dp", None),
    )
    return jax.shard_map(
        per_device,
        mesh=mesh,
        in_specs=placed,
        out_specs=(P("section", "dp", None), P("section")),
        check_vma=False,
    )
```

time: 64.8 us -> 52.8 us (0.81)
  Pallas kernels: 56.8 us -> 48.4 us
  local copies, waits for them, and re-layouts: 5.43 us -> 1.88 us
    pallas_call x1, Pallas kernels: 56.8 us -> 48.4 us  [per_device(): pl.pallas_call(functools.partial(relay, sections, shards, chunk, group),...]
    unnamed x3 -> x1, local copies, waits for them, and re-layouts: 5.43 us -> 1.88 us
where the time goes in v2:
time: 52.8 us; the launch traced here: 52.7 us
  Pallas kernels  48.4 us (92%)
  between operations  2.34 us (4%)
  local copies, waits for them, and re-layouts  1.88 us (4%)
    pallas_call x1, Pallas kernels, per_device(): pl.pallas_call(functools.partial(relay, sections, shards, chunk, group),...  48.4 us
    unnamed x1, local copies, waits for them, and re-layouts  1.88 us

profile of v2, /device:TPU:3, one launch (start us, length us, event | category | flops | bytes accessed | tf_op | source)
XLA Modules:
  0.0 52.7 jit_solution(7221255011459132330)
XLA Ops:
  0.6 48.4 %shard_map.77 = (bf16[2,64,2048]{2,1,0:T(8,128)(2,1)}, f32[1]{0:T(128)}) custom-call(bf16[8,64,2048]{2,1,0:T(8,128)(2,1)} %hidden.1, bf16[1,2048]{1,0:T(2,128)(2,1)} %gain.1, bf16[60,2048]{1,0:T(8,128)(2,1)} %bitcast.4, bf16[1,60,2048]{2,1,0:T(8,128)(2,1)} %scale.1, bf16[1,2048,2048]{2,1,0:T(8,128)(2,1)} %mix.1, s32[1,8,4,64]{3,2,1,0:T(4,128)} %bitcast.5), custom_call_target="tpu_custom_call" | custom-call | tf_op jit(solution)/shard_map/pallas_call | solution.py:250
  49.1 1.9 %copy.10 = bf16[2,64,2048]{2,1,0:T(8,128)(2,1)} copy(bf16[2,64,2048]{2,1,0:T(8,128)(2,1)} %get-tuple-element.4) | data formatting | bytes 1048576

commit v3 on v2

--- a/solution.py
+++ b/solution.py
@@ -30,7 +30,6 @@
     scale_v,
     gain_v,
     routes_v,
-    normed_v,
     normed_b,
     mixed_v,
     stats,
@@ -129,7 +128,6 @@
         for at in range(0, width, 256):
             part = arrived[at_group, :, at : at + 256].astype(jnp.float32)
             normed = part * inverse * gain_v[:, at : at + 256].astype(jnp.float32)
-            normed_v[:, at : at + 256] = normed
             normed_b[:, at : at + 256] = normed.astype(jnp.bfloat16)
         logits = lax.dot_general(
             normed_b[...],
@@ -143,11 +141,13 @@
         stats[0:1, 0:experts] += jnp.sum(onehot, axis=0, keepdims=True)
         stats[1:2, 0:experts] += jnp.sum(probabilities, axis=0, keepdims=True)
 
-        for at in range(0, width, 256):
+        for at in range(0, width, chunk):
             channel = jnp.dot(
-                gates, scale_v[:, at : at + 256], preferred_element_type=jnp.float32
+                gates, scale_v[:, at : at + chunk], preferred_element_type=jnp.float32
             )
-            mixed_v[:, at : at + 256] = (normed_v[:, at : at + 256] * channel).astype(jnp.bfloat16)
+            part = arrived[at_group, :, at : at + chunk].astype(jnp.float32)
+            normed = part * inverse * gain_v[:, at : at + chunk].astype(jnp.float32)
+            mixed_v[:, at : at + chunk] = (normed * channel).astype(jnp.bfloat16)
 
         @pl.when(at_group == groups - 1)
         def _():
@@ -244,7 +244,7 @@
     picks = routes.shape[3]
     group = 2 if batches % 2 == 0 else 1
     groups, tall = batches // group, group * rows
-    chunk = 256
+    chunk = 512
     pieces = width // chunk
     anywhere = pl.BlockSpec(memory_space=pl.ANY)
     return pl.pallas_call(
@@ -263,7 +263,6 @@
             pltpu.VMEM((experts, width), jnp.bfloat16),
             pltpu.VMEM((1, width), jnp.bfloat16),
             pltpu.VMEM((batches, picks, rows), jnp.int32),
-            pltpu.VMEM((tall, width), jnp.float32),
             pltpu.VMEM((tall, width), jnp.bfloat16),
             pltpu.VMEM((tall, width), jnp.bfloat16),
             pltpu.VMEM((8, 128), jnp.float32),

time: 52.8 us -> 49.4 us (0.936)
  Pallas kernels: 48.4 us -> 45 us
    pallas_call x1, Pallas kernels: 48.4 us -> 45 us  [per_device(): pl.pallas_call(functools.partial(relay, sections, shards, chunk, group),...]
where the time goes in v3:
time: 49.4 us; the launch traced here: 49.3 us
  Pallas kernels  45 us (91%)
  between operations  2.34 us (5%)
  local copies, waits for them, and re-layouts  1.88 us (4%)
    pallas_call x1, Pallas kernels, per_device(): pl.pallas_call(functools.partial(relay, sections, shards, chunk, group),...  45 us
    unnamed x1, local copies, waits for them, and re-layouts  1.88 us

profile of v3, /device:TPU:3, one launch (start us, length us, event | category | flops | bytes accessed | tf_op | source)
XLA Modules:
  0.0 49.3 jit_solution(15868703027961192185)
XLA Ops:
  0.6 45.0 %shard_map.77 = (bf16[2,64,2048]{2,1,0:T(8,128)(2,1)}, f32[1]{0:T(128)}) custom-call(bf16[8,64,2048]{2,1,0:T(8,128)(2,1)} %hidden.1, bf16[1,2048]{1,0:T(2,128)(2,1)} %gain.1, bf16[60,2048]{1,0:T(8,128)(2,1)} %bitcast.4, bf16[1,60,2048]{2,1,0:T(8,128)(2,1)} %scale.1, bf16[1,2048,2048]{2,1,0:T(8,128)(2,1)} %mix.1, s32[1,8,4,64]{3,2,1,0:T(4,128)} %bitcast.5), custom_call_target="tpu_custom_call" | custom-call | tf_op jit(solution)/shard_map/pallas_call | solution.py:250
  45.7 1.9 %copy.10 = bf16[2,64,2048]{2,1,0:T(8,128)(2,1)} copy(bf16[2,64,2048]{2,1,0:T(8,128)(2,1)} %get-tuple-element.4) | data formatting | bytes 1048576

commit v4 on v3

--- a/solution.py
+++ b/solution.py
@@ -242,7 +242,7 @@
     batches, rows, width = hidden_in.shape
     experts = router_weight.shape[2]
     picks = routes.shape[3]
-    group = 2 if batches % 2 == 0 else 1
+    group = 1
     groups, tall = batches // group, group * rows
     chunk = 512
     pieces = width // chunk

time: 49.4 us -> 48.5 us (0.982)
  Pallas kernels: 45 us -> 44.1 us
    pallas_call x1, Pallas kernels: 45 us -> 44.1 us  [per_device(): pl.pallas_call(functools.partial(relay, sections, shards, chunk, group),...]
where the time goes in v4:
time: 48.5 us; the launch traced here: 48.3 us
  Pallas kernels  44.1 us (91%)
  between operations  2.34 us (5%)
  local copies, waits for them, and re-layouts  1.88 us (4%)
    pallas_call x1, Pallas kernels, per_device(): pl.pallas_call(functools.partial(relay, sections, shards, chunk, group),...  44.1 us
    unnamed x1, local copies, waits for them, and re-layouts  1.88 us

profile of v4, /device:TPU:3, one launch (start us, length us, event | category | flops | bytes accessed | tf_op | source)
XLA Modules:
  0.0 48.3 jit_solution(4443427952596107302)
XLA Ops:
  0.6 44.1 %shard_map.77 = (bf16[2,64,2048]{2,1,0:T(8,128)(2,1)}, f32[1]{0:T(128)}) custom-call(bf16[8,64,2048]{2,1,0:T(8,128)(2,1)} %hidden.1, bf16[1,2048]{1,0:T(2,128)(2,1)} %gain.1, bf16[60,2048]{1,0:T(8,128)(2,1)} %bitcast.4, bf16[1,60,2048]{2,1,0:T(8,128)(2,1)} %scale.1, bf16[1,2048,2048]{2,1,0:T(8,128)(2,1)} %mix.1, s32[1,8,4,64]{3,2,1,0:T(4,128)} %bitcast.5), custom_call_target="tpu_custom_call" | custom-call | tf_op jit(solution)/shard_map/pallas_call | solution.py:250
  44.7 1.9 %copy.10 = bf16[2,64,2048]{2,1,0:T(8,128)(2,1)} copy(bf16[2,64,2048]{2,1,0:T(8,128)(2,1)} %get-tuple-element.4) | data formatting | bytes 1048576

commit v5 on v4

--- a/solution.py
+++ b/solution.py
@@ -202,20 +202,20 @@
                         device_id_type=MESH,
                     ).start()
 
+                @pl.when((section == last) & (owner == last))
+                def _():
+                    pltpu.make_async_copy(
+                        left.at[at_group, pl.ds(k * rows, rows), columns],
+                        out.at[lax.rem(batch, owned), :, columns],
+                        out_sem.at[lax.rem(batch, owned)],
+                    ).start()
+
         return carry
 
     lax.fori_loop(0, groups, one_group, 0)
 
-    @pl.when(section == last)
-    def _():
-        for slot in range(owned):
-            batch = batches - owned + slot
-            out[slot] = left[batch // group, pl.ds(batch % group * rows, rows), :]
-
-    @pl.when(section != last)
-    def _():
-        for slot in range(owned):
-            pltpu.make_async_copy(out.at[slot], out.at[slot], out_sem.at[slot]).wait()
+    for slot in range(owned):
+        pltpu.make_async_copy(out.at[slot], out.at[slot], out_sem.at[slot]).wait()
 
     for batch in range(batches):
         sent = left.at[batch // group, pl.ds(batch % group * rows, rows), :]
@@ -254,7 +254,7 @@
             jax.ShapeDtypeStruct((1,), jnp.float32),
         ),
         in_specs=[anywhere] * 6,
-        out_specs=(pl.BlockSpec(memory_space=pltpu.VMEM), pl.BlockSpec(memory_space=pltpu.SMEM)),
+        out_specs=(anywhere, pl.BlockSpec(memory_space=pltpu.SMEM)),
         scratch_shapes=[
             pltpu.VMEM((groups, tall, width), jnp.bfloat16),
             pltpu.VMEM((groups, tall, width), jnp.bfloat16),

time: 48.5 us -> 48.4 us (level)
  no operation moved by 1% of the time
where the time goes in v5:
time: 48.4 us; the launch traced here: 48.2 us
  Pallas kernels  44 us (91%)
  between operations  2.34 us (5%)
  local copies, waits for them, and re-layouts  1.88 us (4%)
    pallas_call x1, Pallas kernels, per_device(): pl.pallas_call(functools.partial(relay, sections, shards, chunk, group),...  44 us
    unnamed x1, local copies, waits for them, and re-layouts  1.88 us

profile of v5, /device:TPU:3, one launch (start us, length us, event | category | flops | bytes accessed | tf_op | source)
XLA Modules:
  0.0 48.2 jit_solution(1822848428884512632)
XLA Ops:
  0.6 44.0 %shard_map.77 = (bf16[2,64,2048]{2,1,0:T(8,128)(2,1)}, f32[1]{0:T(128)}) custom-call(bf16[8,64,2048]{2,1,0:T(8,128)(2,1)} %hidden.1, bf16[1,2048]{1,0:T(2,128)(2,1)} %gain.1, bf16[60,2048]{1,0:T(8,128)(2,1)} %bitcast.4, bf16[1,60,2048]{2,1,0:T(8,128)(2,1)} %scale.1, bf16[1,2048,2048]{2,1,0:T(8,128)(2,1)} %mix.1, s32[1,8,4,64]{3,2,1,0:T(4,128)} %bitcast.5), custom_call_target="tpu_custom_call" | custom-call | tf_op jit(solution)/shard_map/pallas_call | solution.py:250
  44.6 1.9 %copy.10 = bf16[2,64,2048]{2,1,0:T(8,128)(2,1)} copy(bf16[2,64,2048]{2,1,0:T(8,128)(2,1)} %get-tuple-element.4) | data formatting | bytes 1048576
